TPU v7x, 32 devices: a whole 2x2x4 slice. The times are simulated.
32 devices in a mesh: ep: 8 (over z, x), rep: 4 (over y, core).
Axes of the slice: x: 2, y: 2, z: 4, core: 2. Of those that a mesh axis runs over, the one named last changes fastest.
Arguments:
- tension: float32 [4096, 512], P(('rep', 'ep')), parts along dimension 0, may hold values from -6 to 6
- tile_dest: int32 [4096], P(('rep', 'ep')), parts along dimension 0, may hold values from 0 to 1023, as said below
- restriction: float32 [8, 64], replicated, may hold values from -0.75 to 0.75
- elem_block: int32 [32768], P(('rep', 'ep')), parts along dimension 0, may hold values from 0 to 1023
- shared_own: int32 [8192], P(('rep', 'ep')), parts along dimension 0, may hold values from 0 to 1023, as said below
- shared_send: int32 [8192], P(('rep', 'ep')), parts along dimension 0, may hold values from 0 to 1023
Outputs:
- quadrature: float32 [8, 32768], P(None, ('rep', 'ep')), parts along dimension 1
There are 4 independent parts, one for each index of `rep`. A program takes and returns all parts, laid end to end along the dimension named above; an argument that names none is the same for every part. Nothing has to cross between parts.
Inputs may be any that keep to these rules, and one draw needn't show every extreme that they name: `tile_dest`: A permutation of the tile positions. The 128 entries of one device name, for each device's block of 128 positions, either exactly 32 positions in it or none. `shared_own`: the 256 entries of one device are distinct.
All inputs are finite; a program needn't handle non-finite values.
Results may differ from a plain program's by a relative error of at most 0.00007.
Values sent between devices are 32-bit elements; how exact they have to be, the bound alone decides.
A program may use at most 64 MiB of HBM per device.

v0:
```python
import functools

import jax
import jax.numpy as jnp
from jax import lax
from jax.experimental import pallas as pl
from jax.experimental.pallas import tpu as pltpu
from jax.sharding import PartitionSpec as P

F32 = jnp.float32
BF16 = jnp.bfloat16
I32 = jnp.int32
MINOR = (((1,), (1,)), ((), ()))


def iota(shape, dim):
    return lax.broadcasted_iota(I32, shape, dim)


def pieces(x):
    high = x.astype(BF16)
    return high, (x - high.astype(F32)).astype(BF16)


def select_rows(onehot, x):
    lanes = x.shape[1]
    got = jnp.dot(onehot, jnp.concatenate(pieces(x), axis=1), preferred_element_type=F32)
    return got[:, :lanes] + got[:, lanes:]


def lanes_of(x, index):
    return jnp.take_along_axis(x, index, axis=1, mode="promise_in_bounds")


def partner(me, k, n):
    if True:
        return lax.rem(me + k, n)
    bit, peer = 1, 0
    while bit < n:
        have = lax.rem(me // bit, 2)
        peer = peer + bit * (1 - have if k & bit else have)
        bit *= 2
    return peer


def kernel(
    n, cap, *refs
):
    given, out, held = refs[:6], refs[6], refs[7:13]
    outbox, inbox, ghost_out, ghost_in, load_sem, send_sem, recv_sem, ghost_sem = refs[13:]
    dest, send, block, restriction, own, tension = held
    me = lax.axis_index("ep")
    tiles = tension.shape[0]
    quad, nodes = restriction.shape
    width = tension.shape[1] // nodes * quad
    lanes = 2 * width
    rows_e = block.shape[0]
    halves = own.shape[0]
    wide = tiles * halves

    barrier = pltpu.get_barrier_semaphore()
    for k in range(1, n):
        pl.semaphore_signal(barrier, inc=1, device_id={"ep": partner(me, n - k, n)})

    arrive = [pltpu.make_async_copy(a, b, load_sem.at[i]) for i, (a, b) in enumerate(zip(given, held))]
    for i in (5, 0, 3, 1, 2, 4):
        arrive[i].start()

    arrive[0].wait()
    arrive[3].wait()
    arrive[5].wait()
    place = dest[...]
    target = lax.div(place, tiles)
    to_peer = jnp.broadcast_to(target, (n, tiles)) == iota((n, tiles), 0)
    to_peer = to_peer.astype(F32)
    earlier = (iota((tiles, tiles), 0) < iota((tiles, tiles), 1)).astype(F32).astype(BF16)
    before = jnp.dot(to_peer.astype(BF16), earlier, preferred_element_type=F32)
    rank = jnp.sum(before * to_peer, axis=0, keepdims=True).astype(I32)
    slot = target * cap + rank
    slots = n * cap
    pack = (jnp.broadcast_to(slot, (slots, tiles)) == iota((slots, tiles), 0)).astype(F32).astype(BF16)
    at_rank = jnp.broadcast_to(rank, (tiles, tiles)) == lax.rem(iota((tiles, tiles), 0), cap)
    where_to = (to_peer * (lax.rem(place, tiles) + 1).astype(F32)).astype(BF16)
    where_to = lax.dot_general(
        where_to, at_rank.astype(F32).astype(BF16), MINOR, preferred_element_type=F32
    )

    full = (lanes, tension.shape[1])
    weight = jnp.concatenate([restriction[...]] * (full[1] // nodes), axis=1)
    weight = jnp.concatenate([weight] * (lanes // quad), axis=0)
    mine = lax.div(lax.rem(iota(full, 0), width), quad) == lax.div(iota(full, 1), nodes)
    weight = jnp.where(mine, weight, 0.0)
    nodal, nodal_low = pieces(tension[...])
    weight, weight_low = pieces(weight)
    by = functools.partial(lax.dot_general, dimension_numbers=MINOR, preferred_element_type=F32)
    local = by(nodal, weight) + (by(nodal_low, weight) + by(nodal, weight_low))
    packed = select_rows(pack, local)
    first = iota((cap, lanes), 1) < width
    for p in range(n):
        after = (p + 1) % n
        outbox[p, :cap, :] = jnp.where(
            first, packed[p * cap : (p + 1) * cap], packed[after * cap : (after + 1) * cap]
        )
        outbox[p, cap : cap + 1, :] = where_to[p : p + 1]
        outbox[p, cap + 1 : cap + 2, :] = where_to[after : after + 1]

    pl.semaphore_wait(barrier, n - 1)
    copies = []
    for k in range(1, n):
        peer = partner(me, k, n)
        copies.append(
            pltpu.make_async_remote_copy(
                src_ref=outbox.at[peer],
                dst_ref=inbox.at[me],
                send_sem=send_sem.at[k],
                recv_sem=recv_sem.at[k],
                device_id={"ep": peer},
            )
        )
    for copy in copies:
        copy.start()
    arrive[1].wait()
    arrive[2].wait()
    for h in range(halves):
        want = jnp.broadcast_to(send[h : h + 1, :], (rows_e, tiles))
        got = lanes_of(block[...], lax.rem(want, tiles))
        ghost_out[h : h + 1, :] = jnp.sum(
            jnp.where(lax.div(want, tiles) == iota((rows_e, tiles), 0), got, 0),
            axis=0, keepdims=True,
        )
    ghosts = pltpu.make_async_remote_copy(
        src_ref=ghost_out,
        dst_ref=ghost_in,
        send_sem=ghost_sem.at[0],
        recv_sem=ghost_sem.at[1],
        device_id={"ep": lax.rem(me + n - 1, n)},
    )
    ghosts.start()
    inbox[me] = outbox[me]

    arrive[4].wait()
    owned = jnp.concatenate([own[h : h + 1, :] for h in range(halves)], axis=1)
    entry = (iota((rows_e, wide), 1) + 1).astype(F32)
    entry = jnp.where(
        jnp.broadcast_to(lax.div(owned, tiles), (rows_e, wide)) == iota((rows_e, wide), 0), entry, 0.0
    ).astype(BF16)
    column = jnp.broadcast_to(lax.rem(owned, tiles), (tiles, wide)) == iota((tiles, wide), 0)
    shared = lax.dot_general(
        entry, column.astype(F32).astype(BF16), MINOR, preferred_element_type=F32
    ).astype(I32)

    ghosts.wait()
    for copy in copies:
        copy.wait()

    per = tiles // cap
    lane = lax.div(iota((1, tiles), 1), cap)
    onehot = []
    for which in range(2):
        parts = []
        for h in range(slots // tiles):
            pos = jnp.zeros((1, tiles), F32)
            for s in range(per):
                pos = jnp.where(lane == s, inbox[h * per + s, cap + which : cap + which + 1, :], pos)
            pos = jnp.broadcast_to(pos.astype(I32), (tiles, tiles))
            parts.append((pos == iota((tiles, tiles), 0) + 1).astype(F32).astype(BF16))
        onehot.append(jnp.concatenate(parts, axis=1))
    arrived = jnp.concatenate([inbox[s, :cap, :] for s in range(n)], axis=0)
    placed = select_rows(jnp.concatenate(onehot, axis=0), arrived)
    placed = jnp.where(iota((tiles, lanes), 1) < width, placed[:tiles], placed[tiles:]).T

    def values(index, base):
        index = jnp.broadcast_to(index, (quad, tiles))
        blocks = width // quad
        tile, part = lax.div(index, blocks), lax.rem(index, blocks)
        got = lanes_of(placed[base : base + quad], tile)
        for b in range(1, blocks):
            low = base + b * quad
            got = jnp.where(part == b, lanes_of(placed[low : low + quad], tile), got)
        return got

    ghost = [values(ghost_in[h : h + 1, :], width) for h in range(halves)]
    for r in range(rows_e):
        mine = values(block[r : r + 1, :], 0)
        which = jnp.broadcast_to(shared[r : r + 1, :], (quad, tiles))
        number = jnp.maximum(which - 1, 0)
        other = lanes_of(ghost[0], lax.rem(number, tiles))
        for h in range(1, halves):
            other = jnp.where(
                lax.div(number, tiles) == h, lanes_of(ghost[h], lax.rem(number, tiles)), other
            )
        out[:, r * tiles : (r + 1) * tiles] = jnp.where(which > 0, 0.5 * (mine + other), mine)


def per_device(tension, tile_dest, restriction, elem_block, shared_own, shared_send):
    n = lax.axis_size("ep")
    tiles = tension.shape[0]
    cap = 2 * tiles // n
    quad, nodes = restriction.shape
    lanes = 2 * (tension.shape[1] // nodes * quad)
    halves = shared_own.shape[0] // tiles
    given = (
        tile_dest.reshape(1, tiles),
        shared_send.reshape(halves, tiles),
        elem_block.reshape(-1, tiles),
        restriction,
        shared_own.reshape(halves, tiles),
        tension,
    )
    return pl.pallas_call(
        functools.partial(kernel, n, cap),
        out_shape=jax.ShapeDtypeStruct((quad, elem_block.shape[0]), F32),
        in_specs=[pl.BlockSpec(memory_space=pltpu.HBM)] * 6,
        out_specs=pl.BlockSpec(memory_space=pltpu.VMEM),
        scratch_shapes=[pltpu.VMEM(a.shape, a.dtype) for a in given]
        + [
            pltpu.VMEM((n, cap + 2, lanes), F32),
            pltpu.VMEM((n, cap + 2, lanes), F32),
            pltpu.VMEM((halves, tiles), I32),
            pltpu.VMEM((halves, tiles), I32),
            pltpu.SemaphoreType.DMA((6,)),
            pltpu.SemaphoreType.DMA((n,)),
            pltpu.SemaphoreType.DMA((n,)),
            pltpu.SemaphoreType.DMA((2,)),
        ],
        compiler_params=pltpu.CompilerParams(
            collective_id=0, has_side_effects=True, vmem_limit_bytes=16 * 2**20
        ),
    )(*[pltpu.with_memory_space_constraint(a, pltpu.HBM) for a in given])


def solution(mesh):
    return jax.shard_map(
        per_device,
        mesh=mesh,
        in_specs=(
            P(("rep", "ep"), None),
            P(("rep", "ep")),
            P(),
            P(("rep", "ep")),
            P(("rep", "ep")),
            P(("rep", "ep")),
        ),
        out_specs=P(None, ("rep", "ep")),
        check_vma=False,
    )
```

profile of v0, /device:TPU:0, one launch (start us, length us, event | category | flops | bytes accessed | tf_op | source)
XLA Modules:
  0.0 11.0 jit_solution(6744447633307045749)
XLA Ops:
  0.0 10.3 %shard_map.64 = f32[8,1024]{1,0:T(8,128)S(1)} custom-call(s32[1,128]{1,0:T(1,128)} %bitcast.7, s32[2,128]{1,0:T(2,128)} %bitcast.5, s32[8,128]{1,0:T(8,128)} %bitcast.4, f32[8,64]{1,0:T(8,128)} %refs_3_.1, s32[2,128]{1,0:T(2,128)} %bitcast.6, f32[128,512]{1,0:T(8,128)} %refs_5_.1), custom_call_target="tpu_custom_call" | custom-call | tf_op jit(solution)/shard_map/pallas_call | solution.py:210
  10.3 0.6 %copy.8 = f32[8,1024]{1,0:T(8,128)} copy(f32[8,1024]{1,0:T(8,128)S(1)} %shard_map.64) | data formatting | bytes 65536
where the time goes:
time: 11.1 us; the launch traced here: 11 us
  Pallas kernels  10.3 us (93%)
  local copies, waits for them, and re-layouts  0.62 us (6%)
    pallas_call x1, Pallas kernels, per_device(): pl.pallas_call(functools.partial(kernel, n, cap), out_shape=jax.ShapeDtyp...  10.3 us
    unnamed x1, local copies, waits for them, and re-layouts  0.62 us

commit v1 on v0

v1 whole, which is shorter than its diff:
```python
import functools

import jax
import jax.numpy as jnp
from jax import lax
from jax.experimental import pallas as pl
from jax.experimental.pallas import tpu as pltpu
from jax.sharding import PartitionSpec as P

F32 = jnp.float32
BF16 = jnp.bfloat16
I32 = jnp.int32
MINOR = (((1,), (1,)), ((), ()))
DEPTH = 256


def iota(shape, dim):
    return lax.broadcasted_iota(I32, shape, dim)


def pieces(x):
    high = x.astype(BF16)
    return high, (x - high.astype(F32)).astype(BF16)


def onehot(x):
    return x.astype(F32).astype(BF16)


def minor_dot(a, b):
    return lax.dot_general(a, b, MINOR, preferred_element_type=F32)


def lanes_of(x, index):
    return jnp.take_along_axis(x, index, axis=1, mode="promise_in_bounds")


def layout(n, tiles, nodal, nodes):
    cap = 2 * tiles // n
    blocks = nodal // nodes
    groups = min(tiles // cap, blocks)
    return cap, blocks, groups, blocks // groups


def kernel(n, *refs):
    given, out, held = refs[:6], refs[6], refs[7:13]
    outbox, inbox, meta_out, meta_in, ghost_out, ghost_in, load_sem, pair_sem = refs[13:]
    dest, send, block, restriction, own, tension = held
    me = lax.axis_index("ep")
    tiles = tension.shape[0]
    quad, nodes = restriction.shape
    cap, blocks, groups, vectors = layout(n, tiles, tension.shape[1], nodes)
    rows_e = block.shape[0]
    halves = own.shape[0]
    wide = tiles * halves
    slots = n * cap
    cuts = tension.shape[1] // DEPTH

    small = [pltpu.make_async_copy(a, b, load_sem.at[i]) for i, (a, b) in enumerate(zip(given[:5], held[:5]))]
    columns = [
        pltpu.make_async_copy(
            given[5].at[:, c * DEPTH : (c + 1) * DEPTH],
            tension.at[:, c * DEPTH : (c + 1) * DEPTH],
            load_sem.at[5 + c],
        )
        for c in range(cuts)
    ]
    for load in small[:1] + columns + small[1:]:
        load.start()

    barrier = pltpu.get_barrier_semaphore()
    for k in range(1, n):
        pl.semaphore_signal(barrier, inc=1, device_id={"ep": lax.rem(me + n - k, n)})

    def remote(src, dst, sem, peer):
        return pltpu.make_async_remote_copy(
            src_ref=src, dst_ref=dst, send_sem=pair_sem.at[sem], recv_sem=pair_sem.at[sem + 1], device_id={"ep": peer}
        )

    small[0].wait()
    place = dest[...]
    target = lax.div(place, tiles)
    to_peer = (jnp.broadcast_to(target, (n, tiles)) == iota((n, tiles), 0)).astype(F32)
    earlier = onehot(iota((tiles, tiles), 0) < iota((tiles, tiles), 1))
    before = jnp.dot(to_peer.astype(BF16), earlier, preferred_element_type=F32)
    rank = jnp.sum(before * to_peer, axis=0, keepdims=True).astype(I32)
    at_rank = onehot(jnp.broadcast_to(rank, (tiles, tiles)) == lax.rem(iota((tiles, tiles), 0), cap))
    position = (lax.rem(place, tiles) + 1).astype(F32)
    wanted = jnp.concatenate([to_peer * iota((n, tiles), 1).astype(F32), to_peer * position], axis=0)
    wanted = minor_dot(wanted.astype(BF16), at_rank)
    tile_of, where_to = wanted[:n].astype(I32), wanted[n:]
    for p in range(n):
        meta_out[p, 0:1, :] = where_to[p : p + 1]
        meta_out[(p + n - 1) % n, 1:2, :] = where_to[p : p + 1]

    small[3].wait()
    full = (DEPTH // nodes * quad, DEPTH)
    weight = jnp.concatenate([restriction[...]] * (DEPTH // nodes), axis=1)
    weight = jnp.concatenate([weight] * (DEPTH // nodes), axis=0)
    weight = jnp.where(lax.div(iota(full, 0), quad) == lax.div(iota(full, 1), nodes), weight, 0.0)
    weight = jnp.concatenate(pieces(weight), axis=0)

    small[1].wait()
    small[2].wait()
    for h in range(halves):
        want = jnp.broadcast_to(send[h : h + 1, :], (rows_e, tiles))
        got = lanes_of(block[...], lax.rem(want, tiles))
        ghost_out[h : h + 1, :] = jnp.sum(
            jnp.where(lax.div(want, tiles) == iota((rows_e, tiles), 0), got, 0), axis=0, keepdims=True
        )

    def pack():
        local = []
        for c in range(cuts):
            columns[c].wait()
            both = jnp.concatenate(pieces(tension[:, c * DEPTH : (c + 1) * DEPTH]), axis=0)
            part = minor_dot(weight, both)
            local.append(part[: full[0], :tiles] + (part[: full[0], tiles:] + part[full[0] :, :tiles]))
        local = jnp.concatenate(local, axis=0)
        group = lax.div(iota((quad, tiles), 1), cap)
        for p in range(n):
            index = jnp.broadcast_to(tile_of[p : p + 1], (quad, tiles))
            for v in range(vectors):
                low = v * groups * quad
                got = lanes_of(local[low : low + quad], index)
                for g in range(1, groups):
                    low = (v * groups + g) * quad
                    got = jnp.where(group == g, lanes_of(local[low : low + quad], index), got)
                outbox[p, v * quad : (v + 1) * quad, :] = got
                outbox[(p + n - 1) % n, (vectors + v) * quad : (vectors + v + 1) * quad, :] = got

    if not EARLY:
        pack()
    pl.semaphore_wait(barrier, n - 1)
    peers = [lax.rem(me + k, n) for k in range(1, n)]
    for peer in peers:
        remote(meta_out.at[peer], meta_in.at[me], 0, peer).start()
    if not EARLY:
        for peer in peers:
            remote(outbox.at[peer], inbox.at[me], 2, peer).start()
    ghosts = remote(ghost_out, ghost_in, 4, lax.rem(me + n - 1, n))
    ghosts.start()
    if EARLY:
        pack()
        for peer in peers:
            remote(outbox.at[peer], inbox.at[me], 2, peer).start()
    meta_in[me] = meta_out[me]
    inbox[me] = outbox[me]

    small[4].wait()
    owned = jnp.concatenate([own[h : h + 1, :] for h in range(halves)], axis=1)
    entry = (iota((rows_e, wide), 1) + 1).astype(F32)
    entry = jnp.where(
        jnp.broadcast_to(lax.div(owned, tiles), (rows_e, wide)) == iota((rows_e, wide), 0), entry, 0.0
    ).astype(BF16)
    column = jnp.broadcast_to(lax.rem(owned, tiles), (tiles, wide)) == iota((tiles, wide), 0)
    shared = minor_dot(entry, onehot(column)).astype(I32)

    def whole(a, b, sem):
        return remote(a.at[pl.ds(0, n - 1)], b.at[pl.ds(0, n - 1)], sem, lax.rem(me + 1, n))

    ghosts.wait_recv()
    metas = whole(meta_out, meta_in, 0)
    metas.wait_recv()
    per = tiles // cap
    lane = lax.div(iota((1, tiles), 1), cap)
    hits = []
    for kind in range(2):
        parts = []
        for h in range(slots // tiles):
            pos = jnp.zeros((1, tiles), F32)
            for s in range(per):
                pos = jnp.where(lane == s, meta_in[h * per + s, kind : kind + 1, :], pos)
            pos = jnp.broadcast_to(pos.astype(I32), (tiles, tiles))
            parts.append(onehot(pos == iota((tiles, tiles), 0) + 1))
        hits.append(jnp.concatenate(parts, axis=1))
    number = iota((rows_e, slots), 1).astype(F32).astype(BF16)
    came_in = minor_dot(number, jnp.concatenate(hits, axis=0)).astype(I32)

    def find(index, table):
        slot = lanes_of(table, lax.div(index, blocks))
        part = lax.rem(index, blocks)
        return (
            lax.rem(part, groups) * cap + lax.rem(slot, cap),
            lax.div(slot, cap) * vectors + lax.div(part, groups),
        )

    which = jnp.maximum(shared - 1, 0)
    other = jnp.zeros((rows_e, tiles), I32)
    for h in range(halves):
        row = jnp.broadcast_to(ghost_in[h : h + 1, :], (rows_e, tiles))
        other = jnp.where(lax.div(which, tiles) == h, lanes_of(row, lax.rem(which, tiles)), other)
    own_lane, own_vector = find(block[...], came_in[:, :tiles])
    ghost_lane, ghost_vector = find(other, came_in[:, tiles:])

    data = whole(outbox, inbox, 2)
    data.wait_recv()

    def spread(x, r):
        return jnp.broadcast_to(x[r : r + 1, :], (quad, tiles))

    def take(r, lane_at, vector_at, base):
        index, vector = spread(lane_at, r), spread(vector_at, r)

        def step(s, got):
            for v in range(vectors):
                low = base + v * quad
                here = lanes_of(inbox[s, low : low + quad, :], index)
                got = jnp.where(vector == s * vectors + v, here, got)
            return got

        return lax.fori_loop(0, n, step, jnp.zeros((quad, tiles), F32), unroll=n <= 16)

    for r in range(rows_e):
        mine = take(r, own_lane, own_vector, 0)
        theirs = take(r, ghost_lane, ghost_vector, vectors * quad)
        out[:, r * tiles : (r + 1) * tiles] = jnp.where(spread(shared, r) > 0, 0.5 * (mine + theirs), mine)

    ghosts.wait_send()
    metas.wait_send()
    data.wait_send()


EARLY = True


def per_device(tension, tile_dest, restriction, elem_block, shared_own, shared_send):
    n = lax.axis_size("ep")
    tiles = tension.shape[0]
    quad, nodes = restriction.shape
    vectors = layout(n, tiles, tension.shape[1], nodes)[3]
    halves = shared_own.shape[0] // tiles
    given = (
        tile_dest.reshape(1, tiles),
        shared_send.reshape(halves, tiles),
        elem_block.reshape(-1, tiles),
        restriction,
        shared_own.reshape(halves, tiles),
        tension,
    )
    return pl.pallas_call(
        functools.partial(kernel, n),
        out_shape=jax.ShapeDtypeStruct((quad, elem_block.shape[0]), F32),
        in_specs=[pl.BlockSpec(memory_space=pltpu.HBM)] * 6,
        out_specs=pl.BlockSpec(memory_space=pltpu.VMEM),
        scratch_shapes=[pltpu.VMEM(a.shape, a.dtype) for a in given]
        + [
            pltpu.VMEM((n, 2 * vectors * quad, tiles), F32),
            pltpu.VMEM((n, 2 * vectors * quad, tiles), F32),
            pltpu.VMEM((n, 2, tiles), F32),
            pltpu.VMEM((n, 2, tiles), F32),
            pltpu.VMEM((halves, tiles), I32),
            pltpu.VMEM((halves, tiles), I32),
            pltpu.SemaphoreType.DMA((5 + tension.shape[1] // DEPTH,)),
            pltpu.SemaphoreType.DMA((6,)),
        ],
        compiler_params=pltpu.CompilerParams(
            collective_id=0, has_side_effects=True, vmem_limit_bytes=16 * 2**20
        ),
    )(*[pltpu.with_memory_space_constraint(a, pltpu.HBM) for a in given])


def solution(mesh):
    return jax.shard_map(
        per_device,
        mesh=mesh,
        in_specs=(
            P(("rep", "ep"), None),
            P(("rep", "ep")),
            P(),
            P(("rep", "ep")),
            P(("rep", "ep")),
            P(("rep", "ep")),
        ),
        out_specs=P(None, ("rep", "ep")),
        check_vma=False,
    )
```

time: 11.1 us -> 11 us (level)
    pallas_call x1, Pallas kernels: 10.3 us -> 10.2 us  [per_device(): pl.pallas_call(functools.partial(kernel, n), out_shape=jax.ShapeDtypeStru...]
where the time goes in v1:
time: 11 us; the launch traced here: 10.8 us
  Pallas kernels  10.2 us (93%)
  local copies, waits for them, and re-layouts  0.62 us (6%)
    pallas_call x1, Pallas kernels, per_device(): pl.pallas_call(functools.partial(kernel, n), out_shape=jax.ShapeDtypeStru...  10.2 us
    unnamed x1, local copies, waits for them, and re-layouts  0.62 us

profile of v1, /device:TPU:0, one launch (start us, length us, event | category | flops | bytes accessed | tf_op | source)
XLA Modules:
  0.0 10.8 jit_solution(10459735532420771678)
XLA Ops:
  0.0 10.2 %shard_map.64 = f32[8,1024]{1,0:T(8,128)S(1)} custom-call(s32[1,128]{1,0:T(1,128)} %bitcast.7, s32[2,128]{1,0:T(2,128)} %bitcast.5, s32[8,128]{1,0:T(8,128)} %bitcast.4, f32[8,64]{1,0:T(8,128)} %refs_3_.1, s32[2,128]{1,0:T(2,128)} %bitcast.6, f32[128,512]{1,0:T(8,128)} %refs_5_.1), custom_call_target="tpu_custom_call" | custom-call | tf_op jit(solution)/shard_map/pallas_call | solution.py:241
  10.2 0.6 %copy.8 = f32[8,1024]{1,0:T(8,128)} copy(f32[8,1024]{1,0:T(8,128)S(1)} %shard_map.64) | data formatting | bytes 65536

commit v2 on v1

--- a/solution.py
+++ b/solution.py
@@ -42,9 +42,13 @@
     return cap, blocks, groups, blocks // groups
 
 
+def stages(n):
+    return (n // 2 + 1, n - 1)
+
+
 def kernel(n, *refs):
     given, out, held = refs[:6], refs[6], refs[7:13]
-    outbox, inbox, meta_out, meta_in, ghost_out, ghost_in, load_sem, pair_sem = refs[13:]
+    outbox, inbox, meta_out, meta_in, ghost_out, ghost_in, load_sem, pair_sem, entered = refs[13:]
     dest, send, block, restriction, own, tension = held
     me = lax.axis_index("ep")
     tiles = tension.shape[0]
@@ -69,15 +73,46 @@
         load.start()
 
     barrier = pltpu.get_barrier_semaphore()
-    for k in range(1, n):
-        pl.semaphore_signal(barrier, inc=1, device_id={"ep": lax.rem(me + n - k, n)})
-
-    def remote(src, dst, sem, peer):
+
+    def each(first, last, step):
+        lax.fori_loop(first, last, lambda p, _: (step(p), 0)[1], 0)
+
+    each(me + 1, n, lambda p: pl.semaphore_signal(barrier, inc=1, device_id={"ep": p}))
+
+    last = n - 1
+    edges = stages(n)
+    parts_of = [range(a, b) for a, b in zip((0,) + edges, edges + (n,))]
+    count = len(parts_of)
+    my_part = sum((me >= edge).astype(I32) for edge in edges)
+
+    def remote(src, dst, sent, got, peer):
         return pltpu.make_async_remote_copy(
-            src_ref=src, dst_ref=dst, send_sem=pair_sem.at[sem], recv_sem=pair_sem.at[sem + 1], device_id={"ep": peer}
+            src_ref=src, dst_ref=dst, send_sem=pair_sem.at[sent], recv_sem=pair_sem.at[got], device_id={"ep": peer}
         )
 
-    small[0].wait()
+    def send_meta(p):
+        remote(meta_out.at[p], meta_in.at[me], 0, 4 + my_part, p).start()
+
+    def send_data(p):
+        remote(outbox.at[p], inbox.at[me], 1, 4 + count + my_part, p).start()
+
+    def send_both(p):
+        send_meta(p)
+        send_data(p)
+
+    def several(a, b, many, sent, got):
+        return remote(a.at[pl.ds(0, many)], b.at[pl.ds(0, many)], sent, got, lax.rem(me + 1, n))
+
+    ghosts = remote(ghost_out, ghost_in, 2, 3, lax.rem(me + last, n))
+
+    @pl.when(me > 0)
+    def _():
+        pl.semaphore_wait(barrier, me)
+
+    each(0, me, lambda p: pl.semaphore_signal(entered.at[me], inc=1, device_id={"ep": p}))
+
+    for i in (0, 3, 1, 2):
+        small[i].wait()
     place = dest[...]
     target = lax.div(place, tiles)
     to_peer = (jnp.broadcast_to(target, (n, tiles)) == iota((n, tiles), 0)).astype(F32)
@@ -93,15 +128,12 @@
         meta_out[p, 0:1, :] = where_to[p : p + 1]
         meta_out[(p + n - 1) % n, 1:2, :] = where_to[p : p + 1]
 
-    small[3].wait()
     full = (DEPTH // nodes * quad, DEPTH)
     weight = jnp.concatenate([restriction[...]] * (DEPTH // nodes), axis=1)
     weight = jnp.concatenate([weight] * (DEPTH // nodes), axis=0)
     weight = jnp.where(lax.div(iota(full, 0), quad) == lax.div(iota(full, 1), nodes), weight, 0.0)
     weight = jnp.concatenate(pieces(weight), axis=0)
 
-    small[1].wait()
-    small[2].wait()
     for h in range(halves):
         want = jnp.broadcast_to(send[h : h + 1, :], (rows_e, tiles))
         got = lanes_of(block[...], lax.rem(want, tiles))
@@ -110,9 +142,10 @@
         )
 
     def pack():
+        for load in columns:
+            load.wait()
         local = []
         for c in range(cuts):
-            columns[c].wait()
             both = jnp.concatenate(pieces(tension[:, c * DEPTH : (c + 1) * DEPTH]), axis=0)
             part = minor_dot(weight, both)
             local.append(part[: full[0], :tiles] + (part[: full[0], tiles:] + part[full[0] :, :tiles]))
@@ -129,21 +162,29 @@
                 outbox[p, v * quad : (v + 1) * quad, :] = got
                 outbox[(p + n - 1) % n, (vectors + v) * quad : (vectors + v + 1) * quad, :] = got
 
-    if not EARLY:
-        pack()
-    pl.semaphore_wait(barrier, n - 1)
-    peers = [lax.rem(me + k, n) for k in range(1, n)]
-    for peer in peers:
-        remote(meta_out.at[peer], meta_in.at[me], 0, peer).start()
-    if not EARLY:
-        for peer in peers:
-            remote(outbox.at[peer], inbox.at[me], 2, peer).start()
-    ghosts = remote(ghost_out, ghost_in, 4, lax.rem(me + n - 1, n))
-    ghosts.start()
-    if EARLY:
-        pack()
-        for peer in peers:
-            remote(outbox.at[peer], inbox.at[me], 2, peer).start()
+    @pl.when(me > 0)
+    def _():
+        send_meta(0)
+        ghosts.start()
+
+    pack()
+
+    @pl.when(me > 0)
+    def _():
+        send_data(0)
+
+    each(1, me, send_both)
+
+    def up(p):
+        pl.semaphore_wait(entered.at[p], 1)
+        send_both(p)
+
+    each(me + 1, n, up)
+
+    @pl.when(me == 0)
+    def _():
+        ghosts.start()
+
     meta_in[me] = meta_out[me]
     inbox[me] = outbox[me]
 
@@ -156,50 +197,48 @@
     column = jnp.broadcast_to(lax.rem(owned, tiles), (tiles, wide)) == iota((tiles, wide), 0)
     shared = minor_dot(entry, onehot(column)).astype(I32)
 
-    def whole(a, b, sem):
-        return remote(a.at[pl.ds(0, n - 1)], b.at[pl.ds(0, n - 1)], sem, lax.rem(me + 1, n))
-
+    which = jnp.maximum(shared - 1, 0)
     ghosts.wait_recv()
-    metas = whole(meta_out, meta_in, 0)
-    metas.wait_recv()
-    per = tiles // cap
-    lane = lax.div(iota((1, tiles), 1), cap)
-    hits = []
-    for kind in range(2):
-        parts = []
-        for h in range(slots // tiles):
-            pos = jnp.zeros((1, tiles), F32)
-            for s in range(per):
-                pos = jnp.where(lane == s, meta_in[h * per + s, kind : kind + 1, :], pos)
-            pos = jnp.broadcast_to(pos.astype(I32), (tiles, tiles))
-            parts.append(onehot(pos == iota((tiles, tiles), 0) + 1))
-        hits.append(jnp.concatenate(parts, axis=1))
-    number = iota((rows_e, slots), 1).astype(F32).astype(BF16)
-    came_in = minor_dot(number, jnp.concatenate(hits, axis=0)).astype(I32)
-
-    def find(index, table):
-        slot = lanes_of(table, lax.div(index, blocks))
-        part = lax.rem(index, blocks)
-        return (
-            lax.rem(part, groups) * cap + lax.rem(slot, cap),
-            lax.div(slot, cap) * vectors + lax.div(part, groups),
-        )
-
-    which = jnp.maximum(shared - 1, 0)
     other = jnp.zeros((rows_e, tiles), I32)
     for h in range(halves):
         row = jnp.broadcast_to(ghost_in[h : h + 1, :], (rows_e, tiles))
         other = jnp.where(lax.div(which, tiles) == h, lanes_of(row, lax.rem(which, tiles)), other)
-    own_lane, own_vector = find(block[...], came_in[:, :tiles])
-    ghost_lane, ghost_vector = find(other, came_in[:, tiles:])
-
-    data = whole(outbox, inbox, 2)
-    data.wait_recv()
+
+    per = tiles // cap
+    lane = lax.div(iota((1, tiles), 1), cap)
+
+    def came_in(sources):
+        first = sources[0] // per
+        spans = range(first, sources[-1] // per + 1)
+        hits = []
+        for kind in range(2):
+            parts = []
+            for h in spans:
+                pos = jnp.zeros((1, tiles), F32)
+                for s in range(per):
+                    if h * per + s in sources:
+                        pos = jnp.where(lane == s, meta_in[h * per + s, kind : kind + 1, :], pos)
+                pos = jnp.broadcast_to(pos.astype(I32), (tiles, tiles))
+                parts.append(onehot(pos == iota((tiles, tiles), 0) + 1))
+            hits.append(jnp.concatenate(parts, axis=1))
+        number = iota((rows_e, len(spans) * tiles), 1) + (first * tiles + 1)
+        return minor_dot(number.astype(F32).astype(BF16), jnp.concatenate(hits, axis=0)).astype(I32)
+
+    def find(index, table):
+        slot = lanes_of(table, lax.div(index, blocks))
+        part = lax.rem(index, blocks)
+        there = jnp.maximum(slot - 1, 0)
+        vector = lax.div(there, cap) * vectors + lax.div(part, groups)
+        return lax.rem(part, groups) * cap + lax.rem(there, cap), jnp.where(slot > 0, vector, -1)
+
+    def find_all(sources):
+        table = came_in(sources)
+        return find(block[...], table[:, :tiles]) + find(other, table[:, tiles:])
 
     def spread(x, r):
         return jnp.broadcast_to(x[r : r + 1, :], (quad, tiles))
 
-    def take(r, lane_at, vector_at, base):
+    def take(r, lane_at, vector_at, base, first, end, got):
         index, vector = spread(lane_at, r), spread(vector_at, r)
 
         def step(s, got):
@@ -209,19 +248,37 @@
                 got = jnp.where(vector == s * vectors + v, here, got)
             return got
 
-        return lax.fori_loop(0, n, step, jnp.zeros((quad, tiles), F32), unroll=n <= 16)
-
+        return lax.fori_loop(first, end, step, got, unroll=end - first <= 16)
+
+    def take_all(found, first, end, mine, theirs):
+        for r in range(rows_e):
+            mine[r] = take(r, found[0], found[1], 0, first, end, mine[r])
+            theirs[r] = take(r, found[2], found[3], vectors * quad, first, end, theirs[r])
+
+    def arrived(a, b, sent, got, sources):
+        ours = (me >= sources[0]) & (me <= sources[-1])
+        for many, there in ((len(sources) - 1, ours), (len(sources), jnp.logical_not(ours))):
+            if many:
+
+                @pl.when(there)
+                def _():
+                    several(a, b, many, sent, got).wait_recv()
+
+    mine = [jnp.zeros((quad, tiles), F32)] * rows_e
+    theirs = [jnp.zeros((quad, tiles), F32)] * rows_e
+    for i, sources in enumerate(parts_of):
+        arrived(meta_out, meta_in, 0, 4 + i, sources)
+        found = find_all(sources)
+        arrived(outbox, inbox, 1, 4 + count + i, sources)
+        take_all(found, sources[0], sources[-1] + 1, mine, theirs)
     for r in range(rows_e):
-        mine = take(r, own_lane, own_vector, 0)
-        theirs = take(r, ghost_lane, ghost_vector, vectors * quad)
-        out[:, r * tiles : (r + 1) * tiles] = jnp.where(spread(shared, r) > 0, 0.5 * (mine + theirs), mine)
+        out[:, r * tiles : (r + 1) * tiles] = jnp.where(
+            spread(shared, r) > 0, 0.5 * (mine[r] + theirs[r]), mine[r]
+        )
 
     ghosts.wait_send()
-    metas.wait_send()
-    data.wait_send()
-
-
-EARLY = True
+    several(meta_out, meta_in, last, 0, 4).wait_send()
+    several(outbox, inbox, last, 1, 4 + count).wait_send()
 
 
 def per_device(tension, tile_dest, restriction, elem_block, shared_own, shared_send):
@@ -252,7 +309,8 @@
             pltpu.VMEM((halves, tiles), I32),
             pltpu.VMEM((halves, tiles), I32),
             pltpu.SemaphoreType.DMA((5 + tension.shape[1] // DEPTH,)),
-            pltpu.SemaphoreType.DMA((6,)),
+            pltpu.SemaphoreType.DMA((4 + 2 * (len(stages(n)) + 1),)),
+            pltpu.SemaphoreType.REGULAR((n,)),
         ],
         compiler_params=pltpu.CompilerParams(
             collective_id=0, has_side_effects=True, vmem_limit_bytes=16 * 2**20

time: 11 us -> 10.6 us (0.964)
  Pallas kernels: 10.2 us -> 9.84 us
    pallas_call x1, Pallas kernels: 10.2 us -> 9.84 us  [per_device(): pl.pallas_call(functools.partial(kernel, n), out_shape=jax.ShapeDtypeStru...]
where the time goes in v2:
time: 10.6 us; the launch traced here: 10.5 us
  Pallas kernels  9.84 us (93%)
  local copies, waits for them, and re-layouts  0.62 us (6%)
    pallas_call x1, Pallas kernels, per_device(): pl.pallas_call(functools.partial(kernel, n), out_shape=jax.ShapeDtypeStru...  9.84 us
    unnamed x1, local copies, waits for them, and re-layouts  0.62 us

profile of v2, /device:TPU:0, one launch (start us, length us, event | category | flops | bytes accessed | tf_op | source)
XLA Modules:
  0.0 10.5 jit_solution(10279020463439816744)
XLA Ops:
  0.0 9.8 %shard_map.64 = f32[8,1024]{1,0:T(8,128)S(1)} custom-call(s32[1,128]{1,0:T(1,128)} %bitcast.7, s32[2,128]{1,0:T(2,128)} %bitcast.5, s32[8,128]{1,0:T(8,128)} %bitcast.4, f32[8,64]{1,0:T(8,128)} %refs_3_.1, s32[2,128]{1,0:T(2,128)} %bitcast.6, f32[128,512]{1,0:T(8,128)} %refs_5_.1), custom_call_target="tpu_custom_call" | custom-call | tf_op jit(solution)/shard_map/pallas_call | solution.py:298
  9.8 0.6 %copy.8 = f32[8,1024]{1,0:T(8,128)} copy(f32[8,1024]{1,0:T(8,128)S(1)} %shard_map.64) | data formatting | bytes 65536

commit v3 on v2

--- a/solution.py
+++ b/solution.py
@@ -141,38 +141,41 @@
             jnp.where(lax.div(want, tiles) == iota((rows_e, tiles), 0), got, 0), axis=0, keepdims=True
         )
 
-    def pack():
-        for load in columns:
-            load.wait()
-        local = []
-        for c in range(cuts):
-            both = jnp.concatenate(pieces(tension[:, c * DEPTH : (c + 1) * DEPTH]), axis=0)
-            part = minor_dot(weight, both)
-            local.append(part[: full[0], :tiles] + (part[: full[0], tiles:] + part[full[0] :, :tiles]))
-        local = jnp.concatenate(local, axis=0)
-        group = lax.div(iota((quad, tiles), 1), cap)
-        for p in range(n):
-            index = jnp.broadcast_to(tile_of[p : p + 1], (quad, tiles))
-            for v in range(vectors):
-                low = v * groups * quad
-                got = lanes_of(local[low : low + quad], index)
-                for g in range(1, groups):
-                    low = (v * groups + g) * quad
-                    got = jnp.where(group == g, lanes_of(local[low : low + quad], index), got)
-                outbox[p, v * quad : (v + 1) * quad, :] = got
-                outbox[(p + n - 1) % n, (vectors + v) * quad : (vectors + v + 1) * quad, :] = got
-
     @pl.when(me > 0)
     def _():
         send_meta(0)
         ghosts.start()
 
-    pack()
+    for load in columns:
+        load.wait()
+    local = []
+    for c in range(cuts):
+        both = jnp.concatenate(pieces(tension[:, c * DEPTH : (c + 1) * DEPTH]), axis=0)
+        part = minor_dot(weight, both)
+        local.append(part[: full[0], :tiles] + (part[: full[0], tiles:] + part[full[0] :, :tiles]))
+    local = jnp.concatenate(local, axis=0)
+    group = lax.div(iota((quad, tiles), 1), cap)
+
+    def pack(p):
+        index = jnp.broadcast_to(tile_of[p : p + 1], (quad, tiles))
+        for v in range(vectors):
+            low = v * groups * quad
+            got = lanes_of(local[low : low + quad], index)
+            for g in range(1, groups):
+                low = (v * groups + g) * quad
+                got = jnp.where(group == g, lanes_of(local[low : low + quad], index), got)
+            outbox[p, v * quad : (v + 1) * quad, :] = got
+            outbox[(p + n - 1) % n, (vectors + v) * quad : (vectors + v + 1) * quad, :] = got
+
+    pack(0)
+    pack(1)
 
     @pl.when(me > 0)
     def _():
         send_data(0)
 
+    for p in range(2, n):
+        pack(p)
     each(1, me, send_both)
 
     def up(p):
@@ -266,11 +269,15 @@
 
     mine = [jnp.zeros((quad, tiles), F32)] * rows_e
     theirs = [jnp.zeros((quad, tiles), F32)] * rows_e
+    arrived(meta_out, meta_in, 0, 4, parts_of[0])
+    found = find_all(parts_of[0])
     for i, sources in enumerate(parts_of):
-        arrived(meta_out, meta_in, 0, 4 + i, sources)
-        found = find_all(sources)
         arrived(outbox, inbox, 1, 4 + count + i, sources)
+        if i + 1 < count:
+            arrived(meta_out, meta_in, 0, 5 + i, parts_of[i + 1])
         take_all(found, sources[0], sources[-1] + 1, mine, theirs)
+        if i + 1 < count:
+            found = find_all(parts_of[i + 1])
     for r in range(rows_e):
         out[:, r * tiles : (r + 1) * tiles] = jnp.where(
             spread(shared, r) > 0, 0.5 * (mine[r] + theirs[r]), mine[r]

time: 10.6 us -> 10.6 us (level)
  no operation moved by 1% of the time
where the time goes in v3:
time: 10.6 us; the launch traced here: 10.4 us
  Pallas kernels  9.81 us (93%)
  local copies, waits for them, and re-layouts  0.62 us (6%)
    pallas_call x1, Pallas kernels, per_device(): pl.pallas_call(functools.partial(kernel, n), out_shape=jax.ShapeDtypeStru...  9.81 us
    unnamed x1, local copies, waits for them, and re-layouts  0.62 us

profile of v3, /device:TPU:0, one launch (start us, length us, event | category | flops | bytes accessed | tf_op | source)
XLA Modules:
  0.0 10.4 jit_solution(9416637318211496308)
XLA Ops:
  0.0 9.8 %shard_map.64 = f32[8,1024]{1,0:T(8,128)S(1)} custom-call(s32[1,128]{1,0:T(1,128)} %bitcast.7, s32[2,128]{1,0:T(2,128)} %bitcast.5, s32[8,128]{1,0:T(8,128)} %bitcast.4, f32[8,64]{1,0:T(8,128)} %refs_3_.1, s32[2,128]{1,0:T(2,128)} %bitcast.6, f32[128,512]{1,0:T(8,128)} %refs_5_.1), custom_call_target="tpu_custom_call" | custom-call | tf_op jit(solution)/shard_map/pallas_call | solution.py:305
  9.8 0.6 %copy.8 = f32[8,1024]{1,0:T(8,128)} copy(f32[8,1024]{1,0:T(8,128)S(1)} %shard_map.64) | data formatting | bytes 65536

commit v4 on v3

--- a/solution.py
+++ b/solution.py
@@ -12,6 +12,7 @@
 I32 = jnp.int32
 MINOR = (((1,), (1,)), ((), ()))
 DEPTH = 256
+LOADS = 8
 
 
 def iota(shape, dim):
@@ -61,14 +62,9 @@
     cuts = tension.shape[1] // DEPTH
 
     small = [pltpu.make_async_copy(a, b, load_sem.at[i]) for i, (a, b) in enumerate(zip(given[:5], held[:5]))]
-    columns = [
-        pltpu.make_async_copy(
-            given[5].at[:, c * DEPTH : (c + 1) * DEPTH],
-            tension.at[:, c * DEPTH : (c + 1) * DEPTH],
-            load_sem.at[5 + c],
-        )
-        for c in range(cuts)
-    ]
+    rows = tiles // LOADS
+    pieces_of = [pl.ds(c * rows, rows) for c in range(LOADS)]
+    columns = [pltpu.make_async_copy(given[5].at[c], tension.at[c], load_sem.at[5]) for c in pieces_of]
     for load in small[:1] + columns + small[1:]:
         load.start()
 
@@ -105,14 +101,8 @@
 
     ghosts = remote(ghost_out, ghost_in, 2, 3, lax.rem(me + last, n))
 
-    @pl.when(me > 0)
-    def _():
-        pl.semaphore_wait(barrier, me)
-
-    each(0, me, lambda p: pl.semaphore_signal(entered.at[me], inc=1, device_id={"ep": p}))
-
-    for i in (0, 3, 1, 2):
-        small[i].wait()
+    small[0].wait()
+    small[3].wait()
     place = dest[...]
     target = lax.div(place, tiles)
     to_peer = (jnp.broadcast_to(target, (n, tiles)) == iota((n, tiles), 0)).astype(F32)
@@ -134,20 +124,12 @@
     weight = jnp.where(lax.div(iota(full, 0), quad) == lax.div(iota(full, 1), nodes), weight, 0.0)
     weight = jnp.concatenate(pieces(weight), axis=0)
 
-    for h in range(halves):
-        want = jnp.broadcast_to(send[h : h + 1, :], (rows_e, tiles))
-        got = lanes_of(block[...], lax.rem(want, tiles))
-        ghost_out[h : h + 1, :] = jnp.sum(
-            jnp.where(lax.div(want, tiles) == iota((rows_e, tiles), 0), got, 0), axis=0, keepdims=True
-        )
-
     @pl.when(me > 0)
     def _():
+        pl.semaphore_wait(barrier, me)
         send_meta(0)
-        ghosts.start()
-
-    for load in columns:
-        load.wait()
+
+    pltpu.make_async_copy(given[5], tension, load_sem.at[5]).wait()
     local = []
     for c in range(cuts):
         both = jnp.concatenate(pieces(tension[:, c * DEPTH : (c + 1) * DEPTH]), axis=0)
@@ -170,9 +152,20 @@
     pack(0)
     pack(1)
 
+    each(0, jnp.minimum(me, 1), send_data)
+    each(0, me, lambda p: pl.semaphore_signal(entered.at[me], inc=1, device_id={"ep": p}))
+    small[1].wait()
+    small[2].wait()
+    for h in range(halves):
+        want = jnp.broadcast_to(send[h : h + 1, :], (rows_e, tiles))
+        got = lanes_of(block[...], lax.rem(want, tiles))
+        ghost_out[h : h + 1, :] = jnp.sum(
+            jnp.where(lax.div(want, tiles) == iota((rows_e, tiles), 0), got, 0), axis=0, keepdims=True
+        )
+
     @pl.when(me > 0)
     def _():
-        send_data(0)
+        ghosts.start()
 
     for p in range(2, n):
         pack(p)
@@ -315,7 +308,7 @@
             pltpu.VMEM((n, 2, tiles), F32),
             pltpu.VMEM((halves, tiles), I32),
             pltpu.VMEM((halves, tiles), I32),
-            pltpu.SemaphoreType.DMA((5 + tension.shape[1] // DEPTH,)),
+            pltpu.SemaphoreType.DMA((6,)),
             pltpu.SemaphoreType.DMA((4 + 2 * (len(stages(n)) + 1),)),
             pltpu.SemaphoreType.REGULAR((n,)),
         ],

time: 10.6 us -> 10.5 us (level)
  Pallas kernels: 9.81 us -> 9.7 us
    pallas_call x1, Pallas kernels: 9.81 us -> 9.7 us  [per_device(): pl.pallas_call(functools.partial(kernel, n), out_shape=jax.ShapeDtypeStru...]
where the time goes in v4:
time: 10.5 us; the launch traced here: 10.3 us
  Pallas kernels  9.7 us (92%)
  local copies, waits for them, and re-layouts  0.62 us (6%)
    pallas_call x1, Pallas kernels, per_device(): pl.pallas_call(functools.partial(kernel, n), out_shape=jax.ShapeDtypeStru...  9.7 us
    unnamed x1, local copies, waits for them, and re-layouts  0.62 us

profile of v4, /device:TPU:0, one launch (start us, length us, event | category | flops | bytes accessed | tf_op | source)
XLA Modules:
  0.0 10.3 jit_solution(10907601870862232802)
XLA Ops:
  0.0 9.7 %shard_map.64 = f32[8,1024]{1,0:T(8,128)S(1)} custom-call(s32[1,128]{1,0:T(1,128)} %bitcast.7, s32[2,128]{1,0:T(2,128)} %bitcast.5, s32[8,128]{1,0:T(8,128)} %bitcast.4, f32[8,64]{1,0:T(8,128)} %refs_3_.1, s32[2,128]{1,0:T(2,128)} %bitcast.6, f32[128,512]{1,0:T(8,128)} %refs_5_.1), custom_call_target="tpu_custom_call" | custom-call | tf_op jit(solution)/shard_map/pallas_call | solution.py:298
  9.7 0.6 %copy.8 = f32[8,1024]{1,0:T(8,128)} copy(f32[8,1024]{1,0:T(8,128)S(1)} %shard_map.64) | data formatting | bytes 65536

commit v5 on v4

--- a/solution.py
+++ b/solution.py
@@ -13,6 +13,7 @@
 MINOR = (((1,), (1,)), ((), ()))
 DEPTH = 256
 LOADS = 8
+HOLD = 1800
 
 
 def iota(shape, dim):
@@ -169,6 +170,11 @@
 
     for p in range(2, n):
         pack(p)
+
+    @pl.when(lax.rem(lax.axis_index("rep"), 2) == 1)
+    def _():
+        pl.delay(HOLD)
+
     each(1, me, send_both)
 
     def up(p):

time: 10.5 us -> 10.3 us (0.981)
  Pallas kernels: 9.7 us -> 9.52 us
    pallas_call x1, Pallas kernels: 9.7 us -> 9.52 us  [per_device(): pl.pallas_call(functools.partial(kernel, n), out_shape=jax.ShapeDtypeStru...]
where the time goes in v5:
time: 10.3 us; the launch traced here: 10.2 us
  Pallas kernels  9.52 us (92%)
  local copies, waits for them, and re-layouts  0.62 us (6%)
    pallas_call x1, Pallas kernels, per_device(): pl.pallas_call(functools.partial(kernel, n), out_shape=jax.ShapeDtypeStru...  9.52 us
    unnamed x1, local copies, waits for them, and re-layouts  0.62 us

profile of v5, /device:TPU:0, one launch (start us, length us, event | category | flops | bytes accessed | tf_op | source)
XLA Modules:
  0.0 10.2 jit_solution(1413638057301620935)
XLA Ops:
  0.0 9.5 %shard_map.64 = f32[8,1024]{1,0:T(8,128)S(1)} custom-call(s32[1,128]{1,0:T(1,128)} %bitcast.7, s32[2,128]{1,0:T(2,128)} %bitcast.5, s32[8,128]{1,0:T(8,128)} %bitcast.4, f32[8,64]{1,0:T(8,128)} %refs_3_.1, s32[2,128]{1,0:T(2,128)} %bitcast.6, f32[128,512]{1,0:T(8,128)} %refs_5_.1), custom_call_target="tpu_custom_call" | custom-call | tf_op jit(solution)/shard_map/pallas_call | solution.py:304
  9.5 0.6 %copy.8 = f32[8,1024]{1,0:T(8,128)} copy(f32[8,1024]{1,0:T(8,128)S(1)} %shard_map.64) | data formatting | bytes 65536

commit v6 on v5

--- a/solution.py
+++ b/solution.py
@@ -13,7 +13,7 @@
 MINOR = (((1,), (1,)), ((), ()))
 DEPTH = 256
 LOADS = 8
-HOLD = 1800
+HOLD = 1500
 
 
 def iota(shape, dim):
@@ -153,10 +153,13 @@
     pack(0)
     pack(1)
 
-    each(0, jnp.minimum(me, 1), send_data)
-    each(0, me, lambda p: pl.semaphore_signal(entered.at[me], inc=1, device_id={"ep": p}))
+    @pl.when(me > 0)
+    def _():
+        send_data(0)
+
     small[1].wait()
     small[2].wait()
+    each(0, me, lambda p: pl.semaphore_signal(entered.at[me], inc=1, device_id={"ep": p}))
     for h in range(halves):
         want = jnp.broadcast_to(send[h : h + 1, :], (rows_e, tiles))
         got = lanes_of(block[...], lax.rem(want, tiles))

time: 10.3 us -> 10.3 us (level)
  no operation moved by 1% of the time
where the time goes in v6:
time: 10.3 us; the launch traced here: 10.2 us
  Pallas kernels  9.53 us (93%)
  local copies, waits for them, and re-layouts  0.62 us (6%)
    pallas_call x1, Pallas kernels, per_device(): pl.pallas_call(functools.partial(kernel, n), out_shape=jax.ShapeDtypeStru...  9.53 us
    unnamed x1, local copies, waits for them, and re-layouts  0.62 us

profile of v6, /device:TPU:0, one launch (start us, length us, event | category | flops | bytes accessed | tf_op | source)
XLA Modules:
  0.0 10.2 jit_solution(14136018856921807627)
XLA Ops:
  0.0 9.5 %shard_map.64 = f32[8,1024]{1,0:T(8,128)S(1)} custom-call(s32[1,128]{1,0:T(1,128)} %bitcast.7, s32[2,128]{1,0:T(2,128)} %bitcast.5, s32[8,128]{1,0:T(8,128)} %bitcast.4, f32[8,64]{1,0:T(8,128)} %refs_3_.1, s32[2,128]{1,0:T(2,128)} %bitcast.6, f32[128,512]{1,0:T(8,128)} %refs_5_.1), custom_call_target="tpu_custom_call" | custom-call | tf_op jit(solution)/shard_map/pallas_call | solution.py:307
  9.5 0.6 %copy.8 = f32[8,1024]{1,0:T(8,128)} copy(f32[8,1024]{1,0:T(8,128)S(1)} %shard_map.64) | data formatting | bytes 65536

commit v7 on v6

--- a/solution.py
+++ b/solution.py
@@ -12,6 +12,13 @@
 I32 = jnp.int32
 MINOR = (((1,), (1,)), ((), ()))
 DEPTH = 256
+ALONG_LANES = lax.GatherDimensionNumbers(
+    offset_dims=(),
+    collapsed_slice_dims=(1,),
+    start_index_map=(1,),
+    operand_batching_dims=(0,),
+    start_indices_batching_dims=(0,),
+)
 LOADS = 8
 HOLD = 1500
 
@@ -34,7 +41,9 @@
 
 
 def lanes_of(x, index):
-    return jnp.take_along_axis(x, index, axis=1, mode="promise_in_bounds")
+    return lax.gather(
+        x, index[..., None], ALONG_LANES, (1, 1), mode=lax.GatherScatterMode.PROMISE_IN_BOUNDS
+    )
 
 
 def layout(n, tiles, nodal, nodes):
@@ -133,9 +142,9 @@
     pltpu.make_async_copy(given[5], tension, load_sem.at[5]).wait()
     local = []
     for c in range(cuts):
-        both = jnp.concatenate(pieces(tension[:, c * DEPTH : (c + 1) * DEPTH]), axis=0)
-        part = minor_dot(weight, both)
-        local.append(part[: full[0], :tiles] + (part[: full[0], tiles:] + part[full[0] :, :tiles]))
+        high, low = pieces(tension[:, c * DEPTH : (c + 1) * DEPTH])
+        part = minor_dot(weight, high)
+        local.append(part[: full[0]] + (part[full[0] :] + minor_dot(weight[: full[0]], low)))
     local = jnp.concatenate(local, axis=0)
     group = lax.div(iota((quad, tiles), 1), cap)
 

time: 10.3 us -> 10.3 us (level)
  no operation moved by 1% of the time
where the time goes in v7:
time: 10.3 us; the launch traced here: 10.1 us
  Pallas kernels  9.52 us (92%)
  local copies, waits for them, and re-layouts  0.62 us (6%)
    pallas_call x1, Pallas kernels, per_device(): pl.pallas_call(functools.partial(kernel, n), out_shape=jax.ShapeDtypeStru...  9.52 us
    unnamed x1, local copies, waits for them, and re-layouts  0.62 us

profile of v7, /device:TPU:0, one launch (start us, length us, event | category | flops | bytes accessed | tf_op | source)
XLA Modules:
  0.0 10.1 jit_solution(3978656377207871051)
XLA Ops:
  0.0 9.5 %shard_map.64 = f32[8,1024]{1,0:T(8,128)S(1)} custom-call(s32[1,128]{1,0:T(1,128)} %bitcast.7, s32[2,128]{1,0:T(2,128)} %bitcast.5, s32[8,128]{1,0:T(8,128)} %bitcast.4, f32[8,64]{1,0:T(8,128)} %refs_3_.1, s32[2,128]{1,0:T(2,128)} %bitcast.6, f32[128,512]{1,0:T(8,128)} %refs_5_.1), custom_call_target="tpu_custom_call" | custom-call | tf_op jit(solution)/shard_map/pallas_call | solution.py:316
  9.5 0.6 %copy.8 = f32[8,1024]{1,0:T(8,128)} copy(f32[8,1024]{1,0:T(8,128)S(1)} %shard_map.64) | data formatting | bytes 65536

commit v8 on v7

--- a/solution.py
+++ b/solution.py
@@ -75,7 +75,7 @@
     rows = tiles // LOADS
     pieces_of = [pl.ds(c * rows, rows) for c in range(LOADS)]
     columns = [pltpu.make_async_copy(given[5].at[c], tension.at[c], load_sem.at[5]) for c in pieces_of]
-    for load in small[:1] + columns + small[1:]:
+    for load in small[:1] + small[3:4] + columns + small[1:3] + small[4:]:
         load.start()
 
     barrier = pltpu.get_barrier_semaphore()

time: 10.3 us -> 10.2 us (level)
  Pallas kernels: 9.52 us -> 9.38 us
    pallas_call x1, Pallas kernels: 9.52 us -> 9.38 us  [per_device(): pl.pallas_call(functools.partial(kernel, n), out_shape=jax.ShapeDtypeStru...]
where the time goes in v8:
time: 10.2 us; the launch traced here: 10 us
  Pallas kernels  9.38 us (92%)
  local copies, waits for them, and re-layouts  0.62 us (6%)
    pallas_call x1, Pallas kernels, per_device(): pl.pallas_call(functools.partial(kernel, n), out_shape=jax.ShapeDtypeStru...  9.38 us
    unnamed x1, local copies, waits for them, and re-layouts  0.62 us

profile of v8, /device:TPU:0, one launch (start us, length us, event | category | flops | bytes accessed | tf_op | source)
XLA Modules:
  0.0 10.0 jit_solution(6144587718447649158)
XLA Ops:
  0.0 9.4 %shard_map.64 = f32[8,1024]{1,0:T(8,128)S(1)} custom-call(s32[1,128]{1,0:T(1,128)} %bitcast.7, s32[2,128]{1,0:T(2,128)} %bitcast.5, s32[8,128]{1,0:T(8,128)} %bitcast.4, f32[8,64]{1,0:T(8,128)} %refs_3_.1, s32[2,128]{1,0:T(2,128)} %bitcast.6, f32[128,512]{1,0:T(8,128)} %refs_5_.1), custom_call_target="tpu_custom_call" | custom-call | tf_op jit(solution)/shard_map/pallas_call | solution.py:316
  9.4 0.6 %copy.8 = f32[8,1024]{1,0:T(8,128)} copy(f32[8,1024]{1,0:T(8,128)S(1)} %shard_map.64) | data formatting | bytes 65536

commit v9 on v8

--- a/solution.py
+++ b/solution.py
@@ -19,7 +19,7 @@
     operand_batching_dims=(0,),
     start_indices_batching_dims=(0,),
 )
-LOADS = 8
+LOADS = 4
 HOLD = 1500
 
 

time: 10.2 us -> 10.2 us (level)
  no operation moved by 1% of the time
where the time goes in v9:
time: 10.2 us; the launch traced here: 10 us
  Pallas kernels  9.38 us (92%)
  local copies, waits for them, and re-layouts  0.62 us (6%)
    pallas_call x1, Pallas kernels, per_device(): pl.pallas_call(functools.partial(kernel, n), out_shape=jax.ShapeDtypeStru...  9.38 us
    unnamed x1, local copies, waits for them, and re-layouts  0.62 us

profile of v9, /device:TPU:0, one launch (start us, length us, event | category | flops | bytes accessed | tf_op | source)
XLA Modules:
  0.0 10.0 jit_solution(190059335352047471)
XLA Ops:
  0.0 9.4 %shard_map.64 = f32[8,1024]{1,0:T(8,128)S(1)} custom-call(s32[1,128]{1,0:T(1,128)} %bitcast.7, s32[2,128]{1,0:T(2,128)} %bitcast.5, s32[8,128]{1,0:T(8,128)} %bitcast.4, f32[8,64]{1,0:T(8,128)} %refs_3_.1, s32[2,128]{1,0:T(2,128)} %bitcast.6, f32[128,512]{1,0:T(8,128)} %refs_5_.1), custom_call_target="tpu_custom_call" | custom-call | tf_op jit(solution)/shard_map/pallas_call | solution.py:316
  9.4 0.6 %copy.8 = f32[8,1024]{1,0:T(8,128)} copy(f32[8,1024]{1,0:T(8,128)S(1)} %shard_map.64) | data formatting | bytes 65536

commit v10 on v9

--- a/solution.py
+++ b/solution.py
@@ -20,7 +20,7 @@
     start_indices_batching_dims=(0,),
 )
 LOADS = 4
-HOLD = 1500
+HOLD = 2200
 
 
 def iota(shape, dim):

time: 10.2 us -> 10.2 us (level)
  no operation moved by 1% of the time
where the time goes in v10:
time: 10.2 us; the launch traced here: 10 us
  Pallas kernels  9.38 us (92%)
  local copies, waits for them, and re-layouts  0.62 us (6%)
    pallas_call x1, Pallas kernels, per_device(): pl.pallas_call(functools.partial(kernel, n), out_shape=jax.ShapeDtypeStru...  9.38 us
    unnamed x1, local copies, waits for them, and re-layouts  0.62 us

profile of v10, /device:TPU:0, one launch (start us, length us, event | category | flops | bytes accessed | tf_op | source)
XLA Modules:
  0.0 10.0 jit_solution(14201580222725695079)
XLA Ops:
  0.0 9.4 %shard_map.64 = f32[8,1024]{1,0:T(8,128)S(1)} custom-call(s32[1,128]{1,0:T(1,128)} %bitcast.7, s32[2,128]{1,0:T(2,128)} %bitcast.5, s32[8,128]{1,0:T(8,128)} %bitcast.4, f32[8,64]{1,0:T(8,128)} %refs_3_.1, s32[2,128]{1,0:T(2,128)} %bitcast.6, f32[128,512]{1,0:T(8,128)} %refs_5_.1), custom_call_target="tpu_custom_call" | custom-call | tf_op jit(solution)/shard_map/pallas_call | solution.py:316
  9.4 0.6 %copy.8 = f32[8,1024]{1,0:T(8,128)} copy(f32[8,1024]{1,0:T(8,128)S(1)} %shard_map.64) | data formatting | bytes 65536

commit v11 on v8

--- a/solution.py
+++ b/solution.py
@@ -54,7 +54,7 @@
 
 
 def stages(n):
-    return (n // 2 + 1, n - 1)
+    return (n - 2, n - 1)
 
 
 def kernel(n, *refs):

time: 10.2 us -> 10.2 us (level)
  no operation moved by 1% of the time
where the time goes in v11:
time: 10.2 us; the launch traced here: 10 us
  Pallas kernels  9.38 us (92%)
  local copies, waits for them, and re-layouts  0.62 us (6%)
    pallas_call x1, Pallas kernels, per_device(): pl.pallas_call(functools.partial(kernel, n), out_shape=jax.ShapeDtypeStru...  9.38 us
    unnamed x1, local copies, waits for them, and re-layouts  0.62 us

profile of v11, /device:TPU:0, one launch (start us, length us, event | category | flops | bytes accessed | tf_op | source)
XLA Modules:
  0.0 10.0 jit_solution(11876841757462610101)
XLA Ops:
  0.0 9.4 %shard_map.64 = f32[8,1024]{1,0:T(8,128)S(1)} custom-call(s32[1,128]{1,0:T(1,128)} %bitcast.7, s32[2,128]{1,0:T(2,128)} %bitcast.5, s32[8,128]{1,0:T(8,128)} %bitcast.4, f32[8,64]{1,0:T(8,128)} %refs_3_.1, s32[2,128]{1,0:T(2,128)} %bitcast.6, f32[128,512]{1,0:T(8,128)} %refs_5_.1), custom_call_target="tpu_custom_call" | custom-call | tf_op jit(solution)/shard_map/pallas_call | solution.py:316
  9.4 0.6 %copy.8 = f32[8,1024]{1,0:T(8,128)} copy(f32[8,1024]{1,0:T(8,128)S(1)} %shard_map.64) | data formatting | bytes 65536
